TPU v7x, 8 devices: a whole 2x2x1 slice. The times are simulated.
8 devices in a mesh: parts: 2 (over z, y), data: 4 (over x, core).
Axes of the slice: x: 2, y: 2, z: 1, core: 2. Of those that a mesh axis runs over, the one named last changes fastest.
Arguments:
- feats: bfloat16 [2048, 28], P('data')
- labels: int32 [2048], P('data')
- w_in: float32 [28, 64, 50], P(None, 'parts'), parts along dimension 1
- w_out: float32 [64, 50], P('parts'), parts along dimension 0
- mom_in: float32 [28, 64, 50], P(None, 'parts'), parts along dimension 1
- mom_out: float32 [64, 50], P('parts'), parts along dimension 0
Outputs:
- output 1: float32 [28, 64, 50], P(None, 'parts'), parts along dimension 1
- output 2: float32 [64, 50], P('parts'), parts along dimension 0
- output 3: float32 [28, 64, 50], P(None, 'parts'), parts along dimension 1
- output 4: float32 [64, 50], P('parts'), parts along dimension 0
- output 5: float32 [64], P('parts'), parts along dimension 0
There are 2 independent parts. A program takes and returns all parts, laid end to end along the dimension named above; an argument that names none is the same for every part.
All inputs are finite; a program needn't handle non-finite values.
Results may differ from a plain program's by a relative error of at most 0.001.
Values are sent between devices in bfloat16 or wider.
A program may use at most 1 GiB of HBM per device.

v0:
```python
import math
import jax
import jax.numpy as jnp
from jax import lax
from jax.sharding import PartitionSpec as P

LEAPS = 16
PRIOR_VAR = 1.0


def local_terms(x_rows, lab_rows, w_flat, pos_out):
    num_chain, hidden = pos_out.shape
    num_rows = x_rows.shape[0]
    pre_act = jnp.dot(x_rows, w_flat, preferred_element_type=jnp.float32).reshape(num_rows, num_chain, hidden)
    hidden_act = jnp.tanh(pre_act)
    logits = jnp.sum(hidden_act * pos_out, axis=-1)
    residual = lab_rows[:, None] - jax.nn.sigmoid(logits)
    grad_out = jnp.sum(hidden_act * residual[:, :, None], axis=0)
    back_grad = (residual[:, :, None] * pos_out * (1.0 - hidden_act * hidden_act)).astype(jnp.bfloat16)
    grad_in = lax.dot_general(x_rows, back_grad.reshape(num_rows, num_chain * hidden), (((0,), (0,)), ((), ())), preferred_element_type=jnp.float32)
    return grad_in.reshape(w_flat.shape[0], num_chain, hidden), grad_out, logits


def solution(mesh):
    row_spec = P('data', None)
    label_spec = P('data')
    in_spec = P(None, 'parts', None)
    out_spec = P('parts', None)
    chain_spec = P('parts')

    def run_chains(feats, labels, w_in, w_out, mom_in, mom_out):
        num_rows, num_feat = feats.shape
        hidden = w_in.shape[2]
        step_size = 1.0 / math.sqrt(num_rows * (num_feat + hidden))
        half_step = 0.5 * step_size

        def device_body(x_rows, y_rows, pos_in, pos_out, vel_in, vel_out):
            lab_rows = y_rows.astype(jnp.float32)
            num_chain = pos_out.shape[0]

            def log_post_grad(pos_in, pos_out):
                w_flat = pos_in.astype(jnp.bfloat16).reshape(num_feat, num_chain * hidden)
                grad_in, grad_out, logits = local_terms(x_rows, lab_rows, w_flat, pos_out)
                grad_in, grad_out = lax.psum((grad_in, grad_out), 'data')
                return grad_in - pos_in / PRIOR_VAR, grad_out - pos_out / PRIOR_VAR, logits

            def leap_step(step_index, state_now):
                pos_in, pos_out, vel_in, vel_out = state_now
                pos_in = pos_in + step_size * vel_in
                pos_out = pos_out + step_size * vel_out
                grad_in, grad_out, logits = log_post_grad(pos_in, pos_out)
                return pos_in, pos_out, vel_in + step_size * grad_in, vel_out + step_size * grad_out

            grad_in, grad_out, logits = log_post_grad(pos_in, pos_out)
            vel_in = vel_in + half_step * grad_in
            vel_out = vel_out + half_step * grad_out
            pos_in, pos_out, vel_in, vel_out = lax.fori_loop(0, LEAPS - 1, leap_step, (pos_in, pos_out, vel_in, vel_out))
            pos_in = pos_in + step_size * vel_in
            pos_out = pos_out + step_size * vel_out
            grad_in, grad_out, logits = log_post_grad(pos_in, pos_out)
            vel_in = vel_in + half_step * grad_in
            vel_out = vel_out + half_step * grad_out
            row_loss = jnp.sum(jax.nn.softplus(logits) - lab_rows[:, None] * logits, axis=0)
            row_loss = lax.psum(row_loss, 'data')
            energy = row_loss + (jnp.sum(pos_in * pos_in, axis=(0, 2)) + jnp.sum(pos_out * pos_out, axis=1)) / (2.0 * PRIOR_VAR) + 0.5 * (jnp.sum(vel_in * vel_in, axis=(0, 2)) + jnp.sum(vel_out * vel_out, axis=1))
            return pos_in, pos_out, vel_in, vel_out, energy

        mapped = jax.shard_map(device_body, mesh=mesh, in_specs=(row_spec, label_spec, in_spec, out_spec, in_spec, out_spec), out_specs=(in_spec, out_spec, in_spec, out_spec, chain_spec), check_vma=False)
        return mapped(feats, labels, w_in, w_out, mom_in, mom_out)

    return run_chains
```

profile of v0, /device:TPU:0, one launch (start us, length us, event | category | flops | bytes accessed | tf_op | source)
XLA Modules:
  0.0 845.9 jit_solution(8664568217830719928)
XLA Ops:
  18.1 13.5 %psum.50 = f32[32,50]{1,0:T(8,128)S(1)} all-reduce(f32[32,50]{1,0:T(8,128)S(1)} %get-tuple-element.75), channel_id=1, replica_groups=mesh['parts'=2,'data'=4] {'data'}, use_global_device_ids=true, to_apply=%region_3.0 | all-reduce | flops 1600 | bytes 12800 | tf_op jit(solution)/shard_map/psum | solution.py:44
  32.3 16.1 %all-reduce.5.cloned.1.call-done = f32[28,32,50]{2,1,0:T(8,128)} async-done(((f32[28,32,50]{2,1,0:T(8,128)}), f32[28,32,50]{2,1,0:T(8,128)}) %all-reduce.5.cloned.1.call-update) | async-done | bytes 179216 | tf_op jit(solution)/shard_map/psum | solution.py:44
  50.5 735.3 %while.16 = (s32[]{:T(128)}, f32[28,32,50]{2,1,0:T(8,128)}, f32[32,50]{1,0:T(8,128)S(1)}, f32[28,32,50]{2,1,0:T(8,128)}, f32[32,50]{1,0:T(8,128)S(1)}, /*index=5...) while((s32[]{:T(128)}, f32[28,32,50]{2,1,0:T(8,128)}, f32[32,50]{1,0:T(8,128)S(1)}, ...), condition=%wide.region_9.0_spmd, body=%wide.region_4.0_spmd.sunk | while | flops 99493952 | bytes 40270004 | solution.py:57
  82.9 14.5 %all-reduce.9.cloned.1.call-done = f32[28,32,50]{2,1,0:T(8,128)} async-done(((f32[28,32,50]{2,1,0:T(8,128)}), f32[28,32,50]{2,1,0:T(8,128)}) %all-reduce.9.cloned.1.call-update) | async-done | bytes 179216 | tf_op jit(solution)/shard_map/while/body/eval_jaxpr/psum | solution.py:44
  121.3 10.6 %psum.57 = f32[32,50]{1,0:T(8,128)S(1)} all-reduce(f32[32,50]{1,0:T(8,128)S(1)} %reduce_sum.129), channel_id=1, replica_groups=mesh['parts'=2,'data'=4] {'data'}, use_global_device_ids=true, to_apply=%region_8.0 | all-reduce | flops 1600 | bytes 12800 | tf_op jit(solution)/shard_map/while/body/eval_jaxpr/psum | solution.py:44
  131.9 14.5 %all-reduce.9.cloned.1.call-done = f32[28,32,50]{2,1,0:T(8,128)} async-done(((f32[28,32,50]{2,1,0:T(8,128)}), f32[28,32,50]{2,1,0:T(8,128)}) %all-reduce.9.cloned.1.call-update) | async-done | bytes 179216 | tf_op jit(solution)/shard_map/while/body/eval_jaxpr/psum | solution.py:44
  180.9 14.5 %all-reduce.9.cloned.1.call-done = f32[28,32,50]{2,1,0:T(8,128)} async-done(((f32[28,32,50]{2,1,0:T(8,128)}), f32[28,32,50]{2,1,0:T(8,128)}) %all-reduce.9.cloned.1.call-update) | async-done | bytes 179216 | tf_op jit(solution)/shard_map/while/body/eval_jaxpr/psum | solution.py:44
  229.9 14.5 %all-reduce.9.cloned.1.call-done = f32[28,32,50]{2,1,0:T(8,128)} async-done(((f32[28,32,50]{2,1,0:T(8,128)}), f32[28,32,50]{2,1,0:T(8,128)}) %all-reduce.9.cloned.1.call-update) | async-done | bytes 179216 | tf_op jit(solution)/shard_map/while/body/eval_jaxpr/psum | solution.py:44
  268.3 10.6 %psum.57 = f32[32,50]{1,0:T(8,128)S(1)} all-reduce(f32[32,50]{1,0:T(8,128)S(1)} %reduce_sum.129), channel_id=1, replica_groups=mesh['parts'=2,'data'=4] {'data'}, use_global_device_ids=true, to_apply=%region_8.0 | all-reduce | flops 1600 | bytes 12800 | tf_op jit(solution)/shard_map/while/body/eval_jaxpr/psum | solution.py:44
  278.9 14.5 %all-reduce.9.cloned.1.call-done = f32[28,32,50]{2,1,0:T(8,128)} async-done(((f32[28,32,50]{2,1,0:T(8,128)}), f32[28,32,50]{2,1,0:T(8,128)}) %all-reduce.9.cloned.1.call-update) | async-done | bytes 179216 | tf_op jit(solution)/shard_map/while/body/eval_jaxpr/psum | solution.py:44
  328.0 14.5 %all-reduce.9.cloned.1.call-done = f32[28,32,50]{2,1,0:T(8,128)} async-done(((f32[28,32,50]{2,1,0:T(8,128)}), f32[28,32,50]{2,1,0:T(8,128)}) %all-reduce.9.cloned.1.call-update) | async-done | bytes 179216 | tf_op jit(solution)/shard_map/while/body/eval_jaxpr/psum | solution.py:44
  377.0 14.5 %all-reduce.9.cloned.1.call-done = f32[28,32,50]{2,1,0:T(8,128)} async-done(((f32[28,32,50]{2,1,0:T(8,128)}), f32[28,32,50]{2,1,0:T(8,128)}) %all-reduce.9.cloned.1.call-update) | async-done | bytes 179216 | tf_op jit(solution)/shard_map/while/body/eval_jaxpr/psum | solution.py:44
  426.0 14.5 %all-reduce.9.cloned.1.call-done = f32[28,32,50]{2,1,0:T(8,128)} async-done(((f32[28,32,50]{2,1,0:T(8,128)}), f32[28,32,50]{2,1,0:T(8,128)}) %all-reduce.9.cloned.1.call-update) | async-done | bytes 179216 | tf_op jit(solution)/shard_map/while/body/eval_jaxpr/psum | solution.py:44
  464.4 10.6 %psum.57 = f32[32,50]{1,0:T(8,128)S(1)} all-reduce(f32[32,50]{1,0:T(8,128)S(1)} %reduce_sum.129), channel_id=1, replica_groups=mesh['parts'=2,'data'=4] {'data'}, use_global_device_ids=true, to_apply=%region_8.0 | all-reduce | flops 1600 | bytes 12800 | tf_op jit(solution)/shard_map/while/body/eval_jaxpr/psum | solution.py:44
  475.0 14.5 %all-reduce.9.cloned.1.call-done = f32[28,32,50]{2,1,0:T(8,128)} async-done(((f32[28,32,50]{2,1,0:T(8,128)}), f32[28,32,50]{2,1,0:T(8,128)}) %all-reduce.9.cloned.1.call-update) | async-done | bytes 179216 | tf_op jit(solution)/shard_map/while/body/eval_jaxpr/psum | solution.py:44
  524.0 14.5 %all-reduce.9.cloned.1.call-done = f32[28,32,50]{2,1,0:T(8,128)} async-done(((f32[28,32,50]{2,1,0:T(8,128)}), f32[28,32,50]{2,1,0:T(8,128)}) %all-reduce.9.cloned.1.call-update) | async-done | bytes 179216 | tf_op jit(solution)/shard_map/while/body/eval_jaxpr/psum | solution.py:44
  573.0 14.5 %all-reduce.9.cloned.1.call-done = f32[28,32,50]{2,1,0:T(8,128)} async-done(((f32[28,32,50]{2,1,0:T(8,128)}), f32[28,32,50]{2,1,0:T(8,128)}) %all-reduce.9.cloned.1.call-update) | async-done | bytes 179216 | tf_op jit(solution)/shard_map/while/body/eval_jaxpr/psum | solution.py:44
  622.1 14.5 %all-reduce.9.cloned.1.call-done = f32[28,32,50]{2,1,0:T(8,128)} async-done(((f32[28,32,50]{2,1,0:T(8,128)}), f32[28,32,50]{2,1,0:T(8,128)}) %all-reduce.9.cloned.1.call-update) | async-done | bytes 179216 | tf_op jit(solution)/shard_map/while/body/eval_jaxpr/psum | solution.py:44
  660.5 10.6 %psum.57 = f32[32,50]{1,0:T(8,128)S(1)} all-reduce(f32[32,50]{1,0:T(8,128)S(1)} %reduce_sum.129), channel_id=1, replica_groups=mesh['parts'=2,'data'=4] {'data'}, use_global_device_ids=true, to_apply=%region_8.0 | all-reduce | flops 1600 | bytes 12800 | tf_op jit(solution)/shard_map/while/body/eval_jaxpr/psum | solution.py:44
  671.1 14.5 %all-reduce.9.cloned.1.call-done = f32[28,32,50]{2,1,0:T(8,128)} async-done(((f32[28,32,50]{2,1,0:T(8,128)}), f32[28,32,50]{2,1,0:T(8,128)}) %all-reduce.9.cloned.1.call-update) | async-done | bytes 179216 | tf_op jit(solution)/shard_map/while/body/eval_jaxpr/psum | solution.py:44
  720.1 14.5 %all-reduce.9.cloned.1.call-done = f32[28,32,50]{2,1,0:T(8,128)} async-done(((f32[28,32,50]{2,1,0:T(8,128)}), f32[28,32,50]{2,1,0:T(8,128)}) %all-reduce.9.cloned.1.call-update) | async-done | bytes 179216 | tf_op jit(solution)/shard_map/while/body/eval_jaxpr/psum | solution.py:44
  769.1 14.5 %all-reduce.9.cloned.1.call-done = f32[28,32,50]{2,1,0:T(8,128)} async-done(((f32[28,32,50]{2,1,0:T(8,128)}), f32[28,32,50]{2,1,0:T(8,128)}) %all-reduce.9.cloned.1.call-update) | async-done | bytes 179216 | tf_op jit(solution)/shard_map/while/body/eval_jaxpr/psum | solution.py:44
  809.0 11.3 %all-reduce = (f32[32,50]{1,0:T(8,128)S(1)}, f32[32]{0:T(128)S(1)}) all-reduce(f32[32,50]{1,0:T(8,128)S(1)} %reduce_sum.107, f32[32]{0:T(128)} %get-tuple-element.77), channel_id=1, replica_groups=mesh['parts'=2,'data'=4] {'data'}, use_global_device_ids=true, to_apply=%region_13.0 | all-reduce | flops 1632 | bytes 13056 | tf_op jit(solution)/shard_map/psum | solution.py:44
  821.1 14.7 %all-reduce.7.cloned.1.call-done = f32[28,32,50]{2,1,0:T(8,128)} async-done(((f32[28,32,50]{2,1,0:T(8,128)}), f32[28,32,50]{2,1,0:T(8,128)}) %all-reduce.7.cloned.1.call-update) | async-done | bytes 179216 | tf_op jit(solution)/shard_map/psum | solution.py:44
  (391 shorter events, 515.7 us)
Async XLA Ops:
  7.2 41.3 %all-reduce.5.cloned.1.call-start = ((), (), s32[]{:S(2)}) async-start(), calls=%async_computation | async-start | bytes 917504 | tf_op jit(solution)/shard_map/psum | solution.py:44
  16.0 32.4 %copy-start.3 = (f32[28,32,50]{2,1,0:T(8,128)S(1)}, f32[28,32,50]{2,1,0:T(8,128)}, u32[]{:S(2)}) copy-start(f32[28,32,50]{2,1,0:T(8,128)} %param.12) | copy-start | bytes 537604
  50.5 46.8 %all-reduce.9.cloned.1.call-start = ((), (), s32[]{:S(2)}) async-start(), calls=%async_computation.2 | async-start | bytes 917504 | tf_op jit(solution)/shard_map/while/body/eval_jaxpr/psum | solution.py:44
  69.8 29.7 %copy-start.7 = (f32[512]{0:T(512)S(1)}, f32[512]{0:T(512)}, u32[]{:S(2)}) copy-start(f32[512]{0:T(512)} %copy-done.6) | copy-start | bytes 6148 | tf_op jit(solution)/shard_map/while
  99.6 46.8 %all-reduce.9.cloned.1.call-start = ((), (), s32[]{:S(2)}) async-start(), calls=%async_computation.2 | async-start | bytes 917504 | tf_op jit(solution)/shard_map/while/body/eval_jaxpr/psum | solution.py:44
  118.8 29.7 %copy-start.7 = (f32[512]{0:T(512)S(1)}, f32[512]{0:T(512)}, u32[]{:S(2)}) copy-start(f32[512]{0:T(512)} %copy-done.6) | copy-start | bytes 6148 | tf_op jit(solution)/shard_map/while
  148.6 46.8 %all-reduce.9.cloned.1.call-start = ((), (), s32[]{:S(2)}) async-start(), calls=%async_computation.2 | async-start | bytes 917504 | tf_op jit(solution)/shard_map/while/body/eval_jaxpr/psum | solution.py:44
  167.9 29.7 %copy-start.7 = (f32[512]{0:T(512)S(1)}, f32[512]{0:T(512)}, u32[]{:S(2)}) copy-start(f32[512]{0:T(512)} %copy-done.6) | copy-start | bytes 6148 | tf_op jit(solution)/shard_map/while
  197.6 46.8 %all-reduce.9.cloned.1.call-start = ((), (), s32[]{:S(2)}) async-start(), calls=%async_computation.2 | async-start | bytes 917504 | tf_op jit(solution)/shard_map/while/body/eval_jaxpr/psum | solution.py:44
  216.9 29.7 %copy-start.7 = (f32[512]{0:T(512)S(1)}, f32[512]{0:T(512)}, u32[]{:S(2)}) copy-start(f32[512]{0:T(512)} %copy-done.6) | copy-start | bytes 6148 | tf_op jit(solution)/shard_map/while
  246.6 46.8 %all-reduce.9.cloned.1.call-start = ((), (), s32[]{:S(2)}) async-start(), calls=%async_computation.2 | async-start | bytes 917504 | tf_op jit(solution)/shard_map/while/body/eval_jaxpr/psum | solution.py:44
  295.6 46.8 %all-reduce.9.cloned.1.call-start = ((), (), s32[]{:S(2)}) async-start(), calls=%async_computation.2 | async-start | bytes 917504 | tf_op jit(solution)/shard_map/while/body/eval_jaxpr/psum | solution.py:44
  344.6 46.8 %all-reduce.9.cloned.1.call-start = ((), (), s32[]{:S(2)}) async-start(), calls=%async_computation.2 | async-start | bytes 917504 | tf_op jit(solution)/shard_map/while/body/eval_jaxpr/psum | solution.py:44
  363.9 29.7 %copy-start.7 = (f32[512]{0:T(512)S(1)}, f32[512]{0:T(512)}, u32[]{:S(2)}) copy-start(f32[512]{0:T(512)} %copy-done.6) | copy-start | bytes 6148 | tf_op jit(solution)/shard_map/while
  393.7 46.8 %all-reduce.9.cloned.1.call-start = ((), (), s32[]{:S(2)}) async-start(), calls=%async_computation.2 | async-start | bytes 917504 | tf_op jit(solution)/shard_map/while/body/eval_jaxpr/psum | solution.py:44
  442.7 46.8 %all-reduce.9.cloned.1.call-start = ((), (), s32[]{:S(2)}) async-start(), calls=%async_computation.2 | async-start | bytes 917504 | tf_op jit(solution)/shard_map/while/body/eval_jaxpr/psum | solution.py:44
  491.7 46.8 %all-reduce.9.cloned.1.call-start = ((), (), s32[]{:S(2)}) async-start(), calls=%async_computation.2 | async-start | bytes 917504 | tf_op jit(solution)/shard_map/while/body/eval_jaxpr/psum | solution.py:44
  540.7 46.8 %all-reduce.9.cloned.1.call-start = ((), (), s32[]{:S(2)}) async-start(), calls=%async_computation.2 | async-start | bytes 917504 | tf_op jit(solution)/shard_map/while/body/eval_jaxpr/psum | solution.py:44
  589.7 46.8 %all-reduce.9.cloned.1.call-start = ((), (), s32[]{:S(2)}) async-start(), calls=%async_computation.2 | async-start | bytes 917504 | tf_op jit(solution)/shard_map/while/body/eval_jaxpr/psum | solution.py:44
  609.0 29.7 %copy-start.7 = (f32[512]{0:T(512)S(1)}, f32[512]{0:T(512)}, u32[]{:S(2)}) copy-start(f32[512]{0:T(512)} %copy-done.6) | copy-start | bytes 6148 | tf_op jit(solution)/shard_map/while
  638.7 46.8 %all-reduce.9.cloned.1.call-start = ((), (), s32[]{:S(2)}) async-start(), calls=%async_computation.2 | async-start | bytes 917504 | tf_op jit(solution)/shard_map/while/body/eval_jaxpr/psum | solution.py:44
  687.8 46.8 %all-reduce.9.cloned.1.call-start = ((), (), s32[]{:S(2)}) async-start(), calls=%async_computation.2 | async-start | bytes 917504 | tf_op jit(solution)/shard_map/while/body/eval_jaxpr/psum | solution.py:44
  736.8 46.8 %all-reduce.9.cloned.1.call-start = ((), (), s32[]{:S(2)}) async-start(), calls=%async_computation.2 | async-start | bytes 917504 | tf_op jit(solution)/shard_map/while/body/eval_jaxpr/psum | solution.py:44
  785.8 50.0 %all-reduce.7.cloned.1.call-start = ((), (), s32[]{:S(2)}) async-start(), calls=%async_computation.1 | async-start | bytes 917504 | tf_op jit(solution)/shard_map/psum | solution.py:44
  (30 other events, 417.3 us)
Sparse Core Ops, SparseCore 0:
  18.2 30.2 all-reduce.4
  69.9 27.3 all-reduce.8
  119.0 27.3 all-reduce.8
  168.0 27.3 all-reduce.8
  217.0 27.3 all-reduce.8
  266.0 27.3 all-reduce.8
  315.0 27.3 all-reduce.8
  364.1 27.3 all-reduce.8
  413.1 27.3 all-reduce.8
  462.1 27.3 all-reduce.8
  511.1 27.3 all-reduce.8
  560.1 27.3 all-reduce.8
  609.1 27.3 all-reduce.8
  658.2 27.3 all-reduce.8
  707.2 27.3 all-reduce.8
  756.2 27.3 all-reduce.8
  808.3 27.4 all-reduce.6
where the time goes:
time: 850 us; the launch traced here: 846 us
  waiting for transfers between devices  248 us (29%)
  local copies, waits for them, and re-layouts  188 us (22%)
  blocking collectives  184 us (22%)
  other arithmetic  158 us (19%)
  matrix products  53.1 us (6%)
  between operations  13.8 us (2%)
    psum x17, waiting for transfers between devices, log_post_grad(): grad_in, grad_out = lax.psum((grad_in, grad_out), 'data')  248 us
    psum x17, blocking collectives, log_post_grad(): grad_in, grad_out = lax.psum((grad_in, grad_out), 'data')  184 us
    mul x32, local copies, waits for them, and re-layouts, local_terms(): residual[:, :, None] * pos_out * (1.0 - hidden_act * hidden_act)  107 us
    reduce_sum x16, other arithmetic, local_terms(): logits = jnp.sum(hidden_act * pos_out, axis=-1)  42.7 us
    dot_general x17, matrix products, local_terms(): lax.dot_general(x_rows, back_grad.reshape(num_rows, num_chain * hidden),...  41.4 us
    reduce_sum x17, other arithmetic, local_terms(): grad_out = jnp.sum(hidden_act * residual[:, :, None], axis=0)  39 us
    add x15, other arithmetic, leap_step(): vel_in + step_size * grad_in  33.2 us
    tanh x16, local copies, waits for them, and re-layouts, local_terms(): hidden_act = jnp.tanh(pre_act)  32.2 us
  transfers between devices with their start and end apart: 17, of which 17 were waited for; matrix products, arithmetic and copies ran while one was open for 5% of the time, Pallas kernels for 0%

commit v1 on v0

v1 whole, which is shorter than its diff:
```python
import functools
import math

import jax
import jax.numpy as jnp
from jax import lax
from jax.experimental import pallas as pl
from jax.experimental.pallas import tpu as pltpu
from jax.sharding import PartitionSpec as P

LEAPS = 16
PRIOR_VAR = 1.0
MESH = pl.DeviceIdType.MESH
f32 = jnp.float32
bf16 = jnp.bfloat16

GROUPS = 2
CHUNK = 256
DP = 32
HP = 64
LEAD = 2


def cat2(x):
    return jnp.concatenate([x, x], axis=1)


def kernel(dims, feats, labels, w_in, w_out, mom_in, mom_out, end_w, end_wo, end_p, end_po, end_e,
           xs, ls, wsl, psl, wos, pos, xsend, xrecv, lrecv, xf, yb, w1, w2, p1, p2,
           zb, act, slope, bgr, accw, araw, gpart, packw, packp, recvw, recvp,
           in_sem, sx, rx, sl, rl, sw, rw, sp, rp):
    D, H, rows_dev, n_rows, eps, half = dims
    G4 = 4
    NT = G4 * H // 8
    R = NT * 8
    NC = n_rows // CHUNK
    U = GROUPS * NC
    me = lax.axis_index("data")
    xi = me // 2
    ci = me % 2
    peers = {1: xi * 2 + (1 - ci), 2: (1 - xi) * 2 + ci, 3: (1 - xi) * 2 + (1 - ci)}
    mine = pl.ds(pl.multiple_of(me * 8, 8), 8)

    copies = [
        pltpu.make_async_copy(feats, xs, in_sem.at[0]),
        pltpu.make_async_copy(labels, ls, in_sem.at[1]),
        pltpu.make_async_copy(w_in.at[:, mine, :], wsl, in_sem.at[2]),
        pltpu.make_async_copy(mom_in.at[:, mine, :], psl, in_sem.at[3]),
        pltpu.make_async_copy(w_out.at[mine, :], wos, in_sem.at[4]),
        pltpu.make_async_copy(mom_out.at[mine, :], pos, in_sem.at[5]),
    ]
    for c in copies:
        c.start()
    barrier = pltpu.get_barrier_semaphore()
    for k in peers:
        pl.semaphore_signal(barrier, inc=1, device_id={"data": peers[k]}, device_id_type=MESH)

    copies[0].wait()
    copies[1].wait()
    xf[:, pl.ds(0, rows_dev)] = jnp.zeros((DP, rows_dev), f32)
    xf[pl.ds(0, D), pl.ds(0, rows_dev)] = xs[...].astype(f32)
    xsend[...] = xf[:, pl.ds(0, rows_dev)].astype(bf16)
    pl.semaphore_wait(barrier, 3)
    sends = []
    for k in (2, 3, 1):
        sends.append(pltpu.make_async_remote_copy(src_ref=xsend, dst_ref=xrecv.at[k], send_sem=sx.at[k], recv_sem=rx.at[k],
                                                  device_id={"data": peers[k]}, device_id_type=MESH))
        sends.append(pltpu.make_async_remote_copy(src_ref=ls, dst_ref=lrecv.at[k], send_sem=sl.at[k], recv_sem=rl.at[k],
                                                  device_id={"data": peers[k]}, device_id_type=MESH))
    for s in sends:
        s.start()

    for c in copies[2:]:
        c.wait()
    for ref in (w1, p1):
        ref[...] = jnp.zeros_like(ref)
    for src, dst in ((wsl, w1), (psl, p1)):
        for c in range(8):
            dst[c // 4, pl.ds(c % 4, H, stride=4), pl.ds(0, D)] = src[:, c, :].T
    for src, dst in ((wos, w2), (pos, p2)):
        t = src[...].T
        for c in range(8):
            dst[c // 4, pl.ds(c % 4, H, stride=4), :] = jnp.broadcast_to(t[:, c:c + 1], (H, 128))
    act[3] = jnp.zeros((R, CHUNK), f32)
    slope[3] = jnp.zeros((R, CHUNK), f32)
    accw[1] = jnp.zeros((R, 128), f32)
    gpart[...] = jnp.zeros((R, DP), f32)
    zb[...] = jnp.zeros_like(zb)

    def put_labels(k, lab):
        lab = lab.astype(f32)
        for j in range(rows_dev // 128):
            yb[:, pl.ds(k * rows_dev + j * 128, 128)] = jnp.broadcast_to(lab[j:j + 1, :], (8, 128))

    put_labels(0, ls[...])
    for s in sends:
        s.wait()
    for k in (1, 2, 3):
        xf[:, pl.ds(k * rows_dev, rows_dev)] = xrecv[k].astype(f32)
        put_labels(k, lrecv[k])

    def cols(u):
        return pl.ds((u % NC) * CHUNK, CHUNK)

    def grp(u):
        return (u % U) // NC

    def mm_act(u):
        return jnp.dot(w1[grp(u), pl.ds(0, R), :], xf[:, cols(u)], preferred_element_type=f32)

    def mm_grad(u):
        return lax.dot_general(bgr[u % 2], xf[:, cols(u)], (((1,), (1,)), ((), ())), preferred_element_type=f32)

    def resid(u):
        return yb[:, cols(u)] - jax.nn.sigmoid(zb[grp(u), :, cols(u)])

    def forward(u, pre):
        g, s = grp(u), u % 4
        z = None
        for h in range(NT):
            rows = pl.ds(h * 8, 8)
            wo = cat2(w2[g, rows, :])
            a = jnp.tanh(pre[h * 8:(h + 1) * 8, :])
            t = a * wo
            z = t if z is None else z + t
            act[s, rows, :] = a
            slope[s, rows, :] = wo - t * a
        zb[g, :, cols(u)] = z + pltpu.roll(z, 4, 0)

    def backward(u, r):
        g, s = grp(u), u % 4
        for h in range(NT):
            rows = pl.ds(h * 8, 8)
            ra = r * act[s, rows, :]
            ra = ra[:, :128] + ra[:, 128:]
            if u % NC == 0:
                accw[g, rows, :] = ra
            else:
                accw[g, rows, :] += ra
            bgr[u % 2, rows, :] = r * slope[s, rows, :]

    def update(g, grad, e, f):
        rows = pl.ds(0, R)
        w = w1[g, rows, :]
        p = p1[g, rows, :] + e * (grad - w / PRIOR_VAR)
        p1[g, rows, :] = p
        w1[g, rows, :] = w + f * p
        gw = jnp.sum(accw[g], axis=1, keepdims=True)
        w = w2[g, rows, :]
        p = p2[g, rows, :] + e * (gw - w / PRIOR_VAR)
        p2[g, rows, :] = p
        w2[g, rows, :] = w + f * p

    def slots(first, final, e_prev, f_prev, e_now, f_now, after_first=None):
        ahead = {}
        grad = None
        for s in range(U):
            if not (final and s + LEAD >= U):
                ahead[s + LEAD] = mm_act(s + LEAD)
            u = (s - 1) % U
            r = resid(u)
            forward(s, araw[s] if s < LEAD else ahead.pop(s))
            backward(u, r)
            g = mm_grad(u)
            if s == 0:
                update(1, gpart[...] + g, e_prev, f_prev)
                if after_first is not None:
                    after_first()
            else:
                grad = g if grad is None else grad + g
                if s == NC:
                    update(0, grad, e_now, f_now)
                    grad = None
        return ahead, grad

    for k in range(LEAD):
        araw[k] = mm_act(k)

    def step(i, carry):
        e_prev = jnp.where(i == 0, 0.0, jnp.where(i == 1, half, eps))
        f_prev = jnp.where(i == 0, 0.0, eps)
        e_now = jnp.where(i == 0, half, eps)
        ahead, grad = slots(False, False, e_prev, f_prev, e_now, eps)
        for k in range(LEAD):
            araw[k] = ahead[U + k]
        gpart[...] = grad
        return carry

    lax.fori_loop(0, LEAPS, step, 0)

    def pack(src, src_o, dst):
        for c in range(8):
            m = src[c // 4, pl.ds(c % 4, HP, stride=4), :]
            t = m.T
            dst[pl.ds(c, 16, stride=8), :] = jnp.concatenate([t[0:16], t[16:32]], axis=1)
        lane = lax.broadcasted_iota(jnp.int32, (HP, 128), 1)
        m = jnp.zeros((HP, 128), f32)
        for c in range(8):
            m = jnp.where(lane == c + 8, src_o[c // 4, pl.ds(c % 4, HP, stride=4), :], m)
        return m

    def place_out(m, dst):
        t = m.T
        dst[pl.ds(12 * 8, 8), pl.ds(64, 64)] = t[8:16, :]

    def send_pack(src, dst, ss, rs):
        out = []
        for k in (2, 3, 1):
            c = pltpu.make_async_remote_copy(src_ref=src, dst_ref=dst.at[k], send_sem=ss.at[k], recv_sem=rs.at[k],
                                             device_id={"data": peers[k]}, device_id_type=MESH)
            c.start()
            out.append(c)
        return out

    state = {}

    def send_positions():
        place_out(pack(w1, w2, packw), packw)
        state["w"] = send_pack(packw, recvw, sw, rw)

    ahead, grad = slots(False, True, eps, eps, half, 0.0, send_positions)
    r = resid(U - 1)
    backward(U - 1, r)
    update(1, grad + mm_grad(U - 1), half, 0.0)

    sub = lax.broadcasted_iota(jnp.int32, (8, 128), 0)
    lane = lax.broadcasted_iota(jnp.int32, (8, 128), 1)
    parts = []
    for g in range(GROUPS):
        z = zb[g]
        loss = jnp.maximum(z, 0.0) + jnp.log1p(jnp.exp(-jnp.abs(z))) - yb[...] * z
        rows = pl.ds(0, R)
        sq = w1[g, rows, :] * w1[g, rows, :] / PRIOR_VAR + p1[g, rows, :] * p1[g, rows, :]
        sqo = w2[g, rows, :] * w2[g, rows, :] / PRIOR_VAR + p2[g, rows, :] * p2[g, rows, :]
        sq = jnp.sum(sq.reshape(NT, 8, DP), axis=0)
        sqo = jnp.sum(sqo.reshape(NT, 8, 128), axis=0)
        quad = jnp.sum(sq, axis=1, keepdims=True) + sqo
        quad = quad + pltpu.roll(quad, 4, 0)
        parts.append(jnp.sum(loss, axis=1, keepdims=True) + 0.5 * quad)
    ener = jnp.where(sub < 4, parts[0], parts[1])
    ener = jnp.sum(jnp.where(sub == lane % 8, ener, 0.0), axis=0, keepdims=True)
    place_out(pack(p1, p2, packp), packp)
    packp[pl.ds(15 * 8, 8), pl.ds(64, 64)] = jnp.broadcast_to(ener[:, 0:64], (8, 64))
    state["p"] = send_pack(packp, recvp, sp, rp)

    lane1 = lax.broadcasted_iota(jnp.int32, (1, 128), 1)

    def unpack(q, slab, out3, out2):
        rows = pl.ds(pl.multiple_of(q * 8, 8), 8)
        for j in range(16):
            v = slab[pl.ds(j * 8, 8), :]
            out3[j, rows, :] = v[:, 0:H]
            if j + 16 < D:
                out3[j + 16, rows, :] = pltpu.roll(v, 64, 1)[:, 0:H]
            elif j + 16 == D:
                out2[rows, :] = pltpu.roll(v, 64, 1)[:, 0:H]

    def energy_of(q, slab, cur):
        v = pltpu.roll(slab[pl.ds(15 * 8, 8), :], 64, 1)[0:1, :]
        return jnp.where(lane1 // 8 == q, v, cur)

    unpack(me, packw, end_w, end_wo)
    unpack(me, packp, end_p, end_po)
    en = energy_of(me, packp, jnp.zeros((1, 128), f32))
    for c in state["w"]:
        c.wait()
    for k in (1, 2, 3):
        unpack(peers[k], recvw.at[k], end_w, end_wo)
    for c in state["p"]:
        c.wait()
    for k in (1, 2, 3):
        unpack(peers[k], recvp.at[k], end_p, end_po)
        en = energy_of(peers[k], recvp.at[k], en)
    end_e[...] = en[:, 0:32]


def solution(mesh):
    row_spec = P('data', None)
    label_spec = P('data')
    in_spec = P(None, 'parts', None)
    out_spec = P('parts', None)
    chain_spec = P('parts')

    def run_chains(feats, labels, w_in, w_out, mom_in, mom_out):
        n_rows, D = feats.shape
        H = w_in.shape[2]
        eps = 1.0 / math.sqrt(n_rows * (D + H))

        def device_body(x_rows, y_rows, wi, wo, mi, mo):
            rows_dev = x_rows.shape[0]
            NT = 4 * H // 8
            R = NT * 8
            dims = (D, H, rows_dev, n_rows, eps, 0.5 * eps)
            S = jax.ShapeDtypeStruct
            hbm = pl.BlockSpec(memory_space=pl.ANY)
            vm = pl.BlockSpec(memory_space=pltpu.VMEM)
            V = pltpu.VMEM
            dma = pltpu.SemaphoreType.DMA
            out = pl.pallas_call(
                functools.partial(kernel, dims),
                name='hmc',
                out_shape=[S(wi.shape, f32), S(wo.shape, f32), S(wi.shape, f32), S(wo.shape, f32), S((1, wo.shape[0]), f32)],
                in_specs=[hbm] * 6,
                out_specs=[vm] * 5,
                scratch_shapes=[
                    V((D, rows_dev), bf16), V((rows_dev // 128, 128), jnp.int32),
                    V((D, 8, H), f32), V((D, 8, H), f32), V((8, H), f32), V((8, H), f32),
                    V((DP, rows_dev), bf16), V((4, DP, rows_dev), bf16), V((4, rows_dev // 128, 128), jnp.int32),
                    V((DP, n_rows), f32), V((8, n_rows), f32),
                    V((GROUPS, 4 * HP, DP), f32), V((GROUPS, 4 * HP, 128), f32), V((GROUPS, 4 * HP, DP), f32), V((GROUPS, 4 * HP, 128), f32),
                    V((GROUPS, 8, n_rows), f32),
                    V((4, R, CHUNK), f32), V((4, R, CHUNK), f32), V((2, R, CHUNK), f32), V((GROUPS, R, 128), f32),
                    V((LEAD, R, CHUNK), f32), V((R, DP), f32),
                    V((128, 128), f32), V((128, 128), f32), V((4, 128, 128), f32), V((4, 128, 128), f32),
                    dma((6,)), dma((4,)), dma((4,)), dma((4,)), dma((4,)), dma((4,)), dma((4,)), dma((4,)), dma((4,)),
                ],
                compiler_params=pltpu.CompilerParams(collective_id=0, has_side_effects=True, vmem_limit_bytes=48 * 1024 * 1024),
            )(x_rows.T, y_rows.reshape(rows_dev // 128, 128), wi, wo, mi, mo)
            return out[0], out[1], out[2], out[3], out[4].reshape(-1)

        mapped = jax.shard_map(device_body, mesh=mesh, in_specs=(row_spec, label_spec, in_spec, out_spec, in_spec, out_spec),
                               out_specs=(in_spec, out_spec, in_spec, out_spec, chain_spec), check_vma=False)
        return mapped(feats, labels, w_in, w_out, mom_in, mom_out)

    return run_chains
```

time: 850 us -> 44.4 us (0.05)
  waiting for transfers between devices: 248 us -> 0 us
  blocking collectives: 184 us -> 0 us
  local copies, waits for them, and re-layouts: 188 us -> 8.16 us
  other arithmetic: 158 us -> 0 us
  matrix products: 53.1 us -> 0 us
  Pallas kernels: 0 us -> 35.2 us
  between operations: 13.8 us -> 0.66 us
    psum x17 -> x0, waiting for transfers between devices: 248 us -> none  [log_post_grad(): grad_in, grad_out = lax.psum((grad_in, grad_out), 'data')]
    psum x17 -> x0, blocking collectives: 184 us -> none  [log_post_grad(): grad_in, grad_out = lax.psum((grad_in, grad_out), 'data')]
    mul x48 -> x0, local copies, waits for them, and re-layouts: 119 us -> none  [the longest x32 107 us: local_terms(): residual[:, :, None] * pos_out * (1.0 - hidden_act * hidden_act)]
    reduce_sum x38 -> x0, other arithmetic: 88 us -> none  [the longest x16 42.7 us: local_terms(): logits = jnp.sum(hidden_act * pos_out, axis=-1)]
    dot_general x34 -> x0, matrix products: 53.1 us -> none  [the longest x17 41.4 us: local_terms(): lax.dot_general(x_rows, back_grad.reshape(num_rows, num_chain * hidden),...]
    add x48 -> x0, other arithmetic: 37.4 us -> none  [the longest x15 33.2 us: leap_step(): vel_in + step_size * grad_in]
    pallas_call x0 -> x1, Pallas kernels: none -> 35.2 us  [device_body(): pl.pallas_call(functools.partial(kernel, dims), name='hmc', out_shape=[S(...]
    tanh x16 -> x0, local copies, waits for them, and re-layouts: 32.2 us -> none  [local_terms(): hidden_act = jnp.tanh(pre_act)]
  transfers between devices with their start and end apart: 17 -> 0, of which waited for: 17 -> 0; matrix products, arithmetic and copies ran while one was open for 5% -> 0% of each run, Pallas kernels for 0% -> 0%
where the time goes in v1:
time: 44.4 us; the launch traced here: 44 us
  Pallas kernels  35.2 us (79%)
  local copies, waits for them, and re-layouts  8.16 us (18%)
  between operations  0.66 us (1%)
    pallas_call x1, Pallas kernels, device_body(): pl.pallas_call(functools.partial(kernel, dims), name='hmc', out_shape=[S(...  35.2 us
    unnamed x17, local copies, waits for them, and re-layouts  8.16 us

profile of v1, /device:TPU:0, one launch (start us, length us, event | category | flops | bytes accessed | tf_op | source)
XLA Modules:
  0.0 44.0 jit_solution(14446795823004894142)
XLA Ops:
  0.6 0.0 copy-start.5
  0.6 0.7 %copy-done.5 = s32[512]{0:T(512)S(1)} copy-done((s32[512]{0:T(512)S(1)}, s32[512]{0:T(512)}, u32[]{:S(2)}) %copy-start.5) | copy-done | bytes 2072
  1.3 0.0 copy-start
  1.3 1.0 %copy-done = f32[28,32,50]{2,1,0:T(8,128)S(1)} copy-done((f32[28,32,50]{2,1,0:T(8,128)S(1)}, f32[28,32,50]{2,1,0:T(8,128)}, u32[]{:S(2)}) %copy-start) | copy-done | bytes 179224
  2.3 0.0 copy-start.1
  2.3 1.0 %copy-done.1 = f32[28,32,50]{2,1,0:T(8,128)S(1)} copy-done((f32[28,32,50]{2,1,0:T(8,128)S(1)}, f32[28,32,50]{2,1,0:T(8,128)}, u32[]{:S(2)}) %copy-start.1) | copy-done | bytes 179224
  3.4 0.0 copy-start.2
  3.4 0.8 %copy-done.2 = bf16[512,28]{0,1:T(8,128)(2,1)S(1)} copy-done((bf16[512,28]{0,1:T(8,128)(2,1)S(1)}, bf16[512,28]{0,1:T(8,128)(2,1)}, u32[]{:S(2)}) %copy-start.2) | copy-done | bytes 28696
  4.1 0.0 copy-start.3
  4.1 0.7 %copy-done.3 = f32[32,50]{1,0:T(8,128)S(1)} copy-done((f32[32,50]{1,0:T(8,128)S(1)}, f32[32,50]{1,0:T(8,128)}, u32[]{:S(2)}) %copy-start.3) | copy-done | bytes 6424
  4.8 0.0 copy-start.4
  4.8 0.7 %copy-done.4 = f32[32,50]{1,0:T(8,128)S(1)} copy-done((f32[32,50]{1,0:T(8,128)S(1)}, f32[32,50]{1,0:T(8,128)}, u32[]{:S(2)}) %copy-start.4) | copy-done | bytes 6424
  5.5 35.2 %hmc.1 = (f32[28,32,50]{2,1,0:T(8,128)S(1)}, f32[32,50]{1,0:T(8,128)S(1)}, f32[28,32,50]{2,1,0:T(8,128)S(1)}, f32[32,50]{1,0:T(8,128)S(1)}, f32[1,32]{1,0:T(1,128)S(1)}) custom-call(bf16[28,512]{1,0:T(8,128)(2,1)S(1)} %bitcast.3, s32[4,128]{1,0:T(4,128)S(1)} %bitcast.4, f32[28,32,50]{2,1,0:T(8,128)S(1)} %copy-done, f32[32,50]{1,0:T(8,128)S(1)} %copy-done.3, ...), custom_call_target="tpu_custom_call" | custom-call | tf_op jit(solution)/shard_map/hmc/pallas_call | solution.py:299
  40.7 0.8 %copy.16 = f32[28,32,50]{2,1,0:T(8,128)} copy(f32[28,32,50]{2,1,0:T(8,128)S(1)} %get-tuple-element.20) | data formatting | bytes 358400
  41.5 0.6 %copy.17 = f32[32,50]{1,0:T(8,128)} copy(f32[32,50]{1,0:T(8,128)S(1)} %get-tuple-element.21) | data formatting | bytes 12800
  42.1 0.8 %copy.18 = f32[28,32,50]{2,1,0:T(8,128)} copy(f32[28,32,50]{2,1,0:T(8,128)S(1)} %get-tuple-element.22) | data formatting | bytes 358400
  42.9 0.6 %copy.19 = f32[32,50]{1,0:T(8,128)} copy(f32[32,50]{1,0:T(8,128)S(1)} %get-tuple-element.23) | data formatting | bytes 12800
  43.5 0.5 %copy.20 = f32[32]{0:T(128)} copy(f32[32]{0:T(128)S(1)} %bitcast.5) | data formatting | bytes 256
Async XLA Ops:
  0.6 0.7 %copy-start.5 = (s32[512]{0:T(512)S(1)}, s32[512]{0:T(512)}, u32[]{:S(2)}) copy-start(s32[512]{0:T(512)} %param.7) | copy-start | bytes 6148
  1.3 1.0 %copy-start = (f32[28,32,50]{2,1,0:T(8,128)S(1)}, f32[28,32,50]{2,1,0:T(8,128)}, u32[]{:S(2)}) copy-start(f32[28,32,50]{2,1,0:T(8,128)} %w_in.1) | copy-start | bytes 537604
  2.3 1.0 %copy-start.1 = (f32[28,32,50]{2,1,0:T(8,128)S(1)}, f32[28,32,50]{2,1,0:T(8,128)}, u32[]{:S(2)}) copy-start(f32[28,32,50]{2,1,0:T(8,128)} %mom_in.1) | copy-start | bytes 537604
  3.4 0.8 %copy-start.2 = (bf16[512,28]{0,1:T(8,128)(2,1)S(1)}, bf16[512,28]{0,1:T(8,128)(2,1)}, u32[]{:S(2)}) copy-start(bf16[512,28]{0,1:T(8,128)(2,1)} %param.6) | copy-start | bytes 86020
  4.1 0.7 %copy-start.3 = (f32[32,50]{1,0:T(8,128)S(1)}, f32[32,50]{1,0:T(8,128)}, u32[]{:S(2)}) copy-start(f32[32,50]{1,0:T(8,128)} %w_out.1) | copy-start | bytes 19204
  4.8 0.7 %copy-start.4 = (f32[32,50]{1,0:T(8,128)S(1)}, f32[32,50]{1,0:T(8,128)}, u32[]{:S(2)}) copy-start(f32[32,50]{1,0:T(8,128)} %mom_out.1) | copy-start | bytes 19204

commit v2 on v1

--- a/solution.py
+++ b/solution.py
@@ -274,6 +274,15 @@
     end_e[...] = en[:, 0:32]
 
 
+def store_kernel(*refs):
+    sems = refs[-1]
+    copies = [pltpu.make_async_copy(refs[i], refs[5 + i], sems.at[i]) for i in range(5)]
+    for c in copies:
+        c.start()
+    for c in copies:
+        c.wait()
+
+
 def solution(mesh):
     row_spec = P('data', None)
     label_spec = P('data')
@@ -292,7 +301,7 @@
             R = NT * 8
             dims = (D, H, rows_dev, n_rows, eps, 0.5 * eps)
             S = jax.ShapeDtypeStruct
-            hbm = pl.BlockSpec(memory_space=pl.ANY)
+            hbm = pl.BlockSpec(memory_space=pltpu.HBM)
             vm = pl.BlockSpec(memory_space=pltpu.VMEM)
             V = pltpu.VMEM
             dma = pltpu.SemaphoreType.DMA
@@ -315,7 +324,16 @@
                     dma((6,)), dma((4,)), dma((4,)), dma((4,)), dma((4,)), dma((4,)), dma((4,)), dma((4,)), dma((4,)),
                 ],
                 compiler_params=pltpu.CompilerParams(collective_id=0, has_side_effects=True, vmem_limit_bytes=48 * 1024 * 1024),
-            )(x_rows.T, y_rows.reshape(rows_dev // 128, 128), wi, wo, mi, mo)
+            )(*[pltpu.with_memory_space_constraint(a, pltpu.HBM) for a in (x_rows.T, y_rows.reshape(rows_dev // 128, 128), wi, wo, mi, mo)])
+            out = pl.pallas_call(
+                store_kernel,
+                name='store',
+                out_shape=[S(o.shape, o.dtype) for o in out],
+                in_specs=[vm] * 5,
+                out_specs=[hbm] * 5,
+                scratch_shapes=[dma((5,))],
+                compiler_params=pltpu.CompilerParams(vmem_limit_bytes=4 * 1024 * 1024),
+            )(*out)
             return out[0], out[1], out[2], out[3], out[4].reshape(-1)
 
         mapped = jax.shard_map(device_body, mesh=mesh, in_specs=(row_spec, label_spec, in_spec, out_spec, in_spec, out_spec),

time: 44.4 us -> 36.9 us (0.83)
  local copies, waits for them, and re-layouts: 8.16 us -> 0 us
  Pallas kernels: 35.2 us -> 36.1 us
    unnamed x17 -> x0, local copies, waits for them, and re-layouts: 8.16 us -> none
    pallas_call x0 -> x1, Pallas kernels: none -> 0.97 us  [device_body(): pl.pallas_call(store_kernel, name='store', out_shape=[S(o.shape, o.dtype)...]
where the time goes in v2:
time: 36.9 us; the launch traced here: 36.8 us
  Pallas kernels  36.1 us (98%)
  between operations  0.64 us (2%)
    pallas_call x1, Pallas kernels, device_body(): pl.pallas_call(functools.partial(kernel, dims), name='hmc', out_shape=[S(...  35.1 us
    pallas_call x1, Pallas kernels, device_body(): pl.pallas_call(store_kernel, name='store', out_shape=[S(o.shape, o.dtype)...  0.97 us

profile of v2, /device:TPU:0, one launch (start us, length us, event | category | flops | bytes accessed | tf_op | source)
XLA Modules:
  0.0 36.8 jit_solution(1101864759007227919)
XLA Ops:
  0.6 35.1 %hmc.1 = (f32[28,32,50]{2,1,0:T(8,128)S(1)}, f32[32,50]{1,0:T(8,128)S(1)}, f32[28,32,50]{2,1,0:T(8,128)S(1)}, f32[32,50]{1,0:T(8,128)S(1)}, f32[1,32]{1,0:T(1,128)S(1)}) custom-call(bf16[28,512]{1,0:T(8,128)(2,1)} %bitcast.3, s32[4,128]{1,0:T(4,128)} %bitcast.4, f32[28,32,50]{2,1,0:T(8,128)} %w_in.1, f32[32,50]{1,0:T(8,128)} %w_out.1, f32[28,32,50]{2,1,0:T(8,128)} %mom_in.1, ...), custom_call_target="tpu_custom_call" | custom-call | tf_op jit(solution)/shard_map/hmc/pallas_call | solution.py:308
  35.8 1.0 %store.1 = (f32[28,32,50]{2,1,0:T(8,128)}, f32[32,50]{1,0:T(8,128)}, f32[28,32,50]{2,1,0:T(8,128)}, f32[32,50]{1,0:T(8,128)}, f32[1,32]{1,0:T(1,128)}) custom-call(f32[28,32,50]{2,1,0:T(8,128)S(1)} %get-tuple-element.15.refs_0_, f32[32,50]{1,0:T(8,128)S(1)} %get-tuple-element.16.refs_1_, f32[28,32,50]{2,1,0:T(8,128)S(1)} %get-tuple-element.17.refs_2_, ...), custom_call_target="tpu_custom_call" | custom-call | tf_op jit(solution)/shard_map/store/pallas_call | solution.py:328

commit v3 on v2

--- a/solution.py
+++ b/solution.py
@@ -19,6 +19,8 @@
 DP = 32
 HP = 64
 LEAD = 2
+LAG = 2
+UNROLL = 4
 
 
 def cat2(x):
@@ -81,8 +83,9 @@
         t = src[...].T
         for c in range(8):
             dst[c // 4, pl.ds(c % 4, H, stride=4), :] = jnp.broadcast_to(t[:, c:c + 1], (H, 128))
-    act[3] = jnp.zeros((R, CHUNK), f32)
-    slope[3] = jnp.zeros((R, CHUNK), f32)
+    for u in range(4 - LAG, 4):
+        act[u] = jnp.zeros((R, CHUNK), f32)
+        slope[u] = jnp.zeros((R, CHUNK), f32)
     accw[1] = jnp.zeros((R, 128), f32)
     gpart[...] = jnp.zeros((R, DP), f32)
     zb[...] = jnp.zeros_like(zb)
@@ -109,7 +112,7 @@
         return jnp.dot(w1[grp(u), pl.ds(0, R), :], xf[:, cols(u)], preferred_element_type=f32)
 
     def mm_grad(u):
-        return lax.dot_general(bgr[u % 2], xf[:, cols(u)], (((1,), (1,)), ((), ())), preferred_element_type=f32)
+        return lax.dot_general(bgr[u % 4], xf[:, cols(u)], (((1,), (1,)), ((), ())), preferred_element_type=f32)
 
     def resid(u):
         return yb[:, cols(u)] - jax.nn.sigmoid(zb[grp(u), :, cols(u)])
@@ -137,7 +140,7 @@
                 accw[g, rows, :] = ra
             else:
                 accw[g, rows, :] += ra
-            bgr[u % 2, rows, :] = r * slope[s, rows, :]
+            bgr[u % 4, rows, :] = r * slope[s, rows, :]
 
     def update(g, grad, e, f):
         rows = pl.ds(0, R)
@@ -157,20 +160,22 @@
         for s in range(U):
             if not (final and s + LEAD >= U):
                 ahead[s + LEAD] = mm_act(s + LEAD)
-            u = (s - 1) % U
+            u = (s - LAG) % U
             r = resid(u)
             forward(s, araw[s] if s < LEAD else ahead.pop(s))
             backward(u, r)
             g = mm_grad(u)
             if s == 0:
-                update(1, gpart[...] + g, e_prev, f_prev)
+                grad = gpart[...]
+            grad = g if grad is None else grad + g
+            if s == LAG - 1:
+                update(1, grad, e_prev, f_prev)
+                grad = None
                 if after_first is not None:
                     after_first()
-            else:
-                grad = g if grad is None else grad + g
-                if s == NC:
-                    update(0, grad, e_now, f_now)
-                    grad = None
+            elif s == NC + LAG - 1:
+                update(0, grad, e_now, f_now)
+                grad = None
         return ahead, grad
 
     for k in range(LEAD):
@@ -186,7 +191,7 @@
         gpart[...] = grad
         return carry
 
-    lax.fori_loop(0, LEAPS, step, 0)
+    lax.fori_loop(0, LEAPS, step, 0, unroll=UNROLL)
 
     def pack(src, src_o, dst):
         for c in range(8):
@@ -219,9 +224,10 @@
         state["w"] = send_pack(packw, recvw, sw, rw)
 
     ahead, grad = slots(False, True, eps, eps, half, 0.0, send_positions)
-    r = resid(U - 1)
-    backward(U - 1, r)
-    update(1, grad + mm_grad(U - 1), half, 0.0)
+    for u in range(U - LAG, U):
+        backward(u, resid(u))
+        grad = grad + mm_grad(u)
+    update(1, grad, half, 0.0)
 
     sub = lax.broadcasted_iota(jnp.int32, (8, 128), 0)
     lane = lax.broadcasted_iota(jnp.int32, (8, 128), 1)
@@ -318,7 +324,7 @@
                     V((DP, n_rows), f32), V((8, n_rows), f32),
                     V((GROUPS, 4 * HP, DP), f32), V((GROUPS, 4 * HP, 128), f32), V((GROUPS, 4 * HP, DP), f32), V((GROUPS, 4 * HP, 128), f32),
                     V((GROUPS, 8, n_rows), f32),
-                    V((4, R, CHUNK), f32), V((4, R, CHUNK), f32), V((2, R, CHUNK), f32), V((GROUPS, R, 128), f32),
+                    V((4, R, CHUNK), f32), V((4, R, CHUNK), f32), V((4, R, CHUNK), f32), V((GROUPS, R, 128), f32),
                     V((LEAD, R, CHUNK), f32), V((R, DP), f32),
                     V((128, 128), f32), V((128, 128), f32), V((4, 128, 128), f32), V((4, 128, 128), f32),
                     dma((6,)), dma((4,)), dma((4,)), dma((4,)), dma((4,)), dma((4,)), dma((4,)), dma((4,)), dma((4,)),

time: 36.9 us -> 34.1 us (0.924)
  Pallas kernels: 36.1 us -> 33.4 us
    pallas_call x1, Pallas kernels: 35.1 us -> 32.4 us  [device_body(): pl.pallas_call(functools.partial(kernel, dims), name='hmc', out_shape=[S(...]
where the time goes in v3:
time: 34.1 us; the launch traced here: 34 us
  Pallas kernels  33.4 us (98%)
  between operations  0.64 us (2%)
    pallas_call x1, Pallas kernels, device_body(): pl.pallas_call(functools.partial(kernel, dims), name='hmc', out_shape=[S(...  32.4 us
    pallas_call x1, Pallas kernels, device_body(): pl.pallas_call(store_kernel, name='store', out_shape=[S(o.shape, o.dtype)...  0.97 us

profile of v3, /device:TPU:0, one launch (start us, length us, event | category | flops | bytes accessed | tf_op | source)
XLA Modules:
  0.0 34.0 jit_solution(4811967046943751602)
XLA Ops:
  0.6 32.4 %hmc.1 = (f32[28,32,50]{2,1,0:T(8,128)S(1)}, f32[32,50]{1,0:T(8,128)S(1)}, f32[28,32,50]{2,1,0:T(8,128)S(1)}, f32[32,50]{1,0:T(8,128)S(1)}, f32[1,32]{1,0:T(1,128)S(1)}) custom-call(bf16[28,512]{1,0:T(8,128)(2,1)} %bitcast.3, s32[4,128]{1,0:T(4,128)} %bitcast.4, f32[28,32,50]{2,1,0:T(8,128)} %w_in.1, f32[32,50]{1,0:T(8,128)} %w_out.1, f32[28,32,50]{2,1,0:T(8,128)} %mom_in.1, ...), custom_call_target="tpu_custom_call" | custom-call | tf_op jit(solution)/shard_map/hmc/pallas_call | solution.py:314
  33.0 1.0 %store.1 = (f32[28,32,50]{2,1,0:T(8,128)}, f32[32,50]{1,0:T(8,128)}, f32[28,32,50]{2,1,0:T(8,128)}, f32[32,50]{1,0:T(8,128)}, f32[1,32]{1,0:T(1,128)}) custom-call(f32[28,32,50]{2,1,0:T(8,128)S(1)} %get-tuple-element.15.refs_0_, f32[32,50]{1,0:T(8,128)S(1)} %get-tuple-element.16.refs_1_, f32[28,32,50]{2,1,0:T(8,128)S(1)} %get-tuple-element.17.refs_2_, ...), custom_call_target="tpu_custom_call" | custom-call | tf_op jit(solution)/shard_map/store/pallas_call | solution.py:334

commit v4 on v3

--- a/solution.py
+++ b/solution.py
@@ -20,7 +20,7 @@
 HP = 64
 LEAD = 2
 LAG = 2
-UNROLL = 4
+UNROLL = 8
 
 
 def cat2(x):
@@ -154,7 +154,7 @@
         p2[g, rows, :] = p
         w2[g, rows, :] = w + f * p
 
-    def slots(first, final, e_prev, f_prev, e_now, f_now, after_first=None):
+    def slots(final, e_prev, f_prev, e_now, f_now, after1=None, after0=None):
         ahead = {}
         grad = None
         for s in range(U):
@@ -171,11 +171,13 @@
             if s == LAG - 1:
                 update(1, grad, e_prev, f_prev)
                 grad = None
-                if after_first is not None:
-                    after_first()
+                if after1 is not None:
+                    after1()
             elif s == NC + LAG - 1:
                 update(0, grad, e_now, f_now)
                 grad = None
+                if after0 is not None:
+                    after0()
         return ahead, grad
 
     for k in range(LEAD):
@@ -185,7 +187,7 @@
         e_prev = jnp.where(i == 0, 0.0, jnp.where(i == 1, half, eps))
         f_prev = jnp.where(i == 0, 0.0, eps)
         e_now = jnp.where(i == 0, half, eps)
-        ahead, grad = slots(False, False, e_prev, f_prev, e_now, eps)
+        ahead, grad = slots(False, e_prev, f_prev, e_now, eps)
         for k in range(LEAD):
             araw[k] = ahead[U + k]
         gpart[...] = grad
@@ -193,46 +195,36 @@
 
     lax.fori_loop(0, LEAPS, step, 0, unroll=UNROLL)
 
-    def pack(src, src_o, dst):
-        for c in range(8):
-            m = src[c // 4, pl.ds(c % 4, HP, stride=4), :]
-            t = m.T
-            dst[pl.ds(c, 16, stride=8), :] = jnp.concatenate([t[0:16], t[16:32]], axis=1)
-        lane = lax.broadcasted_iota(jnp.int32, (HP, 128), 1)
-        m = jnp.zeros((HP, 128), f32)
-        for c in range(8):
-            m = jnp.where(lane == c + 8, src_o[c // 4, pl.ds(c % 4, HP, stride=4), :], m)
-        return m
-
-    def place_out(m, dst):
-        t = m.T
-        dst[pl.ds(12 * 8, 8), pl.ds(64, 64)] = t[8:16, :]
-
-    def send_pack(src, dst, ss, rs):
-        out = []
-        for k in (2, 3, 1):
-            c = pltpu.make_async_remote_copy(src_ref=src, dst_ref=dst.at[k], send_sem=ss.at[k], recv_sem=rs.at[k],
-                                             device_id={"data": peers[k]}, device_id_type=MESH)
-            c.start()
-            out.append(c)
-        return out
-
-    state = {}
-
-    def send_positions():
-        place_out(pack(w1, w2, packw), packw)
-        state["w"] = send_pack(packw, recvw, sw, rw)
-
-    ahead, grad = slots(False, True, eps, eps, half, 0.0, send_positions)
-    for u in range(U - LAG, U):
-        backward(u, resid(u))
-        grad = grad + mm_grad(u)
-    update(1, grad, half, 0.0)
-
     sub = lax.broadcasted_iota(jnp.int32, (8, 128), 0)
     lane = lax.broadcasted_iota(jnp.int32, (8, 128), 1)
-    parts = []
-    for g in range(GROUPS):
+    lane_h = lax.broadcasted_iota(jnp.int32, (HP, 128), 1)
+
+    def pack(g, src, src_o, dst):
+        o = jnp.zeros((HP, 128), f32)
+        for c in range(4):
+            rows = pl.ds(c, HP, stride=4)
+            t = src[g, rows, :].T
+            dst[g, pl.ds(c, 16, stride=4), :] = jnp.concatenate([t[0:16], t[16:32]], axis=1)
+            o = jnp.where(lane_h == c, src_o[g, rows, :], o)
+        dst[g, pl.ds(48, 4), pl.ds(64, 64)] = o.T[0:4, :]
+
+    def copy_to(peer, src, dst, ss, rs):
+        return pltpu.make_async_remote_copy(src_ref=src, dst_ref=dst, send_sem=ss, recv_sem=rs,
+                                            device_id={"data": peers[peer]}, device_id_type=MESH)
+
+    def send(g, src, dst, ss, rs, to):
+        out = {}
+        for k in to:
+            out[k] = copy_to(k, src.at[g], dst.at[k, g], ss.at[k, g], rs.at[k, g])
+            out[k].start()
+        return out
+
+    def forward_on(g, dst, ss, rs):
+        c = copy_to(1, dst.at[2, g], dst.at[3, g], ss.at[3, g], rs.at[3, g])
+        c.start()
+        return c
+
+    def energy(g):
         z = zb[g]
         loss = jnp.maximum(z, 0.0) + jnp.log1p(jnp.exp(-jnp.abs(z))) - yb[...] * z
         rows = pl.ds(0, R)
@@ -242,41 +234,73 @@
         sqo = jnp.sum(sqo.reshape(NT, 8, 128), axis=0)
         quad = jnp.sum(sq, axis=1, keepdims=True) + sqo
         quad = quad + pltpu.roll(quad, 4, 0)
-        parts.append(jnp.sum(loss, axis=1, keepdims=True) + 0.5 * quad)
-    ener = jnp.where(sub < 4, parts[0], parts[1])
-    ener = jnp.sum(jnp.where(sub == lane % 8, ener, 0.0), axis=0, keepdims=True)
-    place_out(pack(p1, p2, packp), packp)
-    packp[pl.ds(15 * 8, 8), pl.ds(64, 64)] = jnp.broadcast_to(ener[:, 0:64], (8, 64))
-    state["p"] = send_pack(packp, recvp, sp, rp)
+        return jnp.sum(loss, axis=1, keepdims=True) + 0.5 * quad
+
+    def send_momenta(g, to):
+        packp[g, pl.ds(56, 4), pl.ds(64, 64)] = energy(g)[0:4, 0:64]
+        return send(g, packp, recvp, sp, rp, to)
+
+    sent = {}
+
+    def send_w0():
+        pack(0, w1, w2, packw)
+        sent["w0"] = send(0, packw, recvw, sw, rw, (2, 1))
+
+    def send_w1():
+        pack(1, w1, w2, packw)
+        sent["w1"] = send(1, packw, recvw, sw, rw, (2, 1))
+
+    def send_p0():
+        pack(0, p1, p2, packp)
+        sent["p0"] = send_momenta(0, (2, 1))
+
+    send_w0()
+    ahead, grad = slots(True, eps, eps, half, 0.0, send_w1, send_p0)
+    for u in range(U - LAG, U):
+        backward(u, resid(u))
+        grad = grad + mm_grad(u)
+    update(1, grad, half, 0.0)
+    pack(1, p1, p2, packp)
+    sent["p1"] = send_momenta(1, (2, 3, 1))
 
     lane1 = lax.broadcasted_iota(jnp.int32, (1, 128), 1)
 
-    def unpack(q, slab, out3, out2):
+    def unpack(q, bufs, out3, out2, en):
         rows = pl.ds(pl.multiple_of(q * 8, 8), 8)
-        for j in range(16):
-            v = slab[pl.ds(j * 8, 8), :]
-            out3[j, rows, :] = v[:, 0:H]
-            if j + 16 < D:
-                out3[j + 16, rows, :] = pltpu.roll(v, 64, 1)[:, 0:H]
-            elif j + 16 == D:
-                out2[rows, :] = pltpu.roll(v, 64, 1)[:, 0:H]
-
-    def energy_of(q, slab, cur):
-        v = pltpu.roll(slab[pl.ds(15 * 8, 8), :], 64, 1)[0:1, :]
-        return jnp.where(lane1 // 8 == q, v, cur)
-
-    unpack(me, packw, end_w, end_wo)
-    unpack(me, packp, end_p, end_po)
-    en = energy_of(me, packp, jnp.zeros((1, 128), f32))
-    for c in state["w"]:
-        c.wait()
+        for j in range(8):
+            b0 = bufs[0, pl.ds(j * 8, 8), :]
+            b1 = bufs[1, pl.ds(j * 8, 8), :]
+            for r, v in ((2 * j, jnp.where(sub < 4, b0, pltpu.roll(b1, 4, 0))),
+                         (2 * j + 1, jnp.where(sub < 4, pltpu.roll(b0, 4, 0), b1))):
+                out3[r, rows, :] = v[:, 0:H]
+                if r <= 12 or r == 14:
+                    t = pltpu.roll(v, 64, 1)
+                    if r < 12:
+                        out3[r + 16, rows, :] = t[:, 0:H]
+                    elif r == 12:
+                        out2[rows, :] = t[:, 0:H]
+                    elif en is not None:
+                        t = jnp.sum(jnp.where(sub == lane % 8, t, 0.0), axis=0, keepdims=True)
+                        en = jnp.where(lane1 // 8 == q, t, en)
+        return en
+
+    for name, g in (("w0", 0), ("w1", 1)):
+        sent[name][2].wait()
+        sent[name][3] = forward_on(g, recvw, sw, rw)
+    unpack(me, packw, end_w, end_wo, None)
+    en = unpack(me, packp, end_p, end_po, jnp.zeros((1, 128), f32))
+    sent["p0"][2].wait()
+    sent["p0"][3] = forward_on(0, recvp, sp, rp)
     for k in (1, 2, 3):
-        unpack(peers[k], recvw.at[k], end_w, end_wo)
-    for c in state["p"]:
-        c.wait()
+        for name in ("w0", "w1"):
+            if k != 2:
+                sent[name][k].wait()
+        unpack(peers[k], recvw.at[k], end_w, end_wo, None)
     for k in (1, 2, 3):
-        unpack(peers[k], recvp.at[k], end_p, end_po)
-        en = energy_of(peers[k], recvp.at[k], en)
+        if k != 2:
+            sent["p0"][k].wait()
+        sent["p1"][k].wait()
+        en = unpack(peers[k], recvp.at[k], end_p, end_po, en)
     end_e[...] = en[:, 0:32]
 
 
@@ -326,8 +350,8 @@
                     V((GROUPS, 8, n_rows), f32),
                     V((4, R, CHUNK), f32), V((4, R, CHUNK), f32), V((4, R, CHUNK), f32), V((GROUPS, R, 128), f32),
                     V((LEAD, R, CHUNK), f32), V((R, DP), f32),
-                    V((128, 128), f32), V((128, 128), f32), V((4, 128, 128), f32), V((4, 128, 128), f32),
-                    dma((6,)), dma((4,)), dma((4,)), dma((4,)), dma((4,)), dma((4,)), dma((4,)), dma((4,)), dma((4,)),
+                    V((2, 64, 128), f32), V((2, 64, 128), f32), V((4, 2, 64, 128), f32), V((4, 2, 64, 128), f32),
+                    dma((6,)), dma((4,)), dma((4,)), dma((4,)), dma((4,)), dma((4, 2)), dma((4, 2)), dma((4, 2)), dma((4, 2)),
                 ],
                 compiler_params=pltpu.CompilerParams(collective_id=0, has_side_effects=True, vmem_limit_bytes=48 * 1024 * 1024),
             )(*[pltpu.with_memory_space_constraint(a, pltpu.HBM) for a in (x_rows.T, y_rows.reshape(rows_dev // 128, 128), wi, wo, mi, mo)])

time: 34.1 us -> 31.8 us (0.933)
  Pallas kernels: 33.4 us -> 31.1 us
    pallas_call x1, Pallas kernels: 32.4 us -> 30.1 us  [device_body(): pl.pallas_call(functools.partial(kernel, dims), name='hmc', out_shape=[S(...]
where the time goes in v4:
time: 31.8 us; the launch traced here: 31.7 us
  Pallas kernels  31.1 us (98%)
  between operations  0.64 us (2%)
    pallas_call x1, Pallas kernels, device_body(): pl.pallas_call(functools.partial(kernel, dims), name='hmc', out_shape=[S(...  30.1 us
    pallas_call x1, Pallas kernels, device_body(): pl.pallas_call(store_kernel, name='store', out_shape=[S(o.shape, o.dtype)...  0.97 us

profile of v4, /device:TPU:0, one launch (start us, length us, event | category | flops | bytes accessed | tf_op | source)
XLA Modules:
  0.0 31.7 jit_solution(3093998719028540974)
XLA Ops:
  0.6 30.1 %hmc.1 = (f32[28,32,50]{2,1,0:T(8,128)S(1)}, f32[32,50]{1,0:T(8,128)S(1)}, f32[28,32,50]{2,1,0:T(8,128)S(1)}, f32[32,50]{1,0:T(8,128)S(1)}, f32[1,32]{1,0:T(1,128)S(1)}) custom-call(bf16[28,512]{1,0:T(8,128)(2,1)} %bitcast.3, s32[4,128]{1,0:T(4,128)} %bitcast.4, f32[28,32,50]{2,1,0:T(8,128)} %w_in.1, f32[32,50]{1,0:T(8,128)} %w_out.1, f32[28,32,50]{2,1,0:T(8,128)} %mom_in.1, ...), custom_call_target="tpu_custom_call" | custom-call | tf_op jit(solution)/shard_map/hmc/pallas_call | solution.py:338
  30.7 1.0 %store.1 = (f32[28,32,50]{2,1,0:T(8,128)}, f32[32,50]{1,0:T(8,128)}, f32[28,32,50]{2,1,0:T(8,128)}, f32[32,50]{1,0:T(8,128)}, f32[1,32]{1,0:T(1,128)}) custom-call(f32[28,32,50]{2,1,0:T(8,128)S(1)} %get-tuple-element.15.refs_0_, f32[32,50]{1,0:T(8,128)S(1)} %get-tuple-element.16.refs_1_, f32[28,32,50]{2,1,0:T(8,128)S(1)} %get-tuple-element.17.refs_2_, ...), custom_call_target="tpu_custom_call" | custom-call | tf_op jit(solution)/shard_map/store/pallas_call | solution.py:358

commit v5 on v4

--- a/solution.py
+++ b/solution.py
@@ -96,12 +96,6 @@
             yb[:, pl.ds(k * rows_dev + j * 128, 128)] = jnp.broadcast_to(lab[j:j + 1, :], (8, 128))
 
     put_labels(0, ls[...])
-    for s in sends:
-        s.wait()
-    for k in (1, 2, 3):
-        xf[:, pl.ds(k * rows_dev, rows_dev)] = xrecv[k].astype(f32)
-        put_labels(k, lrecv[k])
-
     def cols(u):
         return pl.ds((u % NC) * CHUNK, CHUNK)
 
@@ -182,6 +176,11 @@
 
     for k in range(LEAD):
         araw[k] = mm_act(k)
+    for s in sends:
+        s.wait()
+    for k in (1, 2, 3):
+        xf[:, pl.ds(k * rows_dev, rows_dev)] = xrecv[k].astype(f32)
+        put_labels(k, lrecv[k])
 
     def step(i, carry):
         e_prev = jnp.where(i == 0, 0.0, jnp.where(i == 1, half, eps))

time: 31.8 us -> 31.7 us (level)
  no operation moved by 1% of the time
where the time goes in v5:
time: 31.7 us; the launch traced here: 31.5 us
  Pallas kernels  30.9 us (97%)
  between operations  0.64 us (2%)
    pallas_call x1, Pallas kernels, device_body(): pl.pallas_call(functools.partial(kernel, dims), name='hmc', out_shape=[S(...  29.9 us
    pallas_call x1, Pallas kernels, device_body(): pl.pallas_call(store_kernel, name='store', out_shape=[S(o.shape, o.dtype)...  0.97 us

profile of v5, /device:TPU:0, one launch (start us, length us, event | category | flops | bytes accessed | tf_op | source)
XLA Modules:
  0.0 31.5 jit_solution(8530012300850663253)
XLA Ops:
  0.6 29.9 %hmc.1 = (f32[28,32,50]{2,1,0:T(8,128)S(1)}, f32[32,50]{1,0:T(8,128)S(1)}, f32[28,32,50]{2,1,0:T(8,128)S(1)}, f32[32,50]{1,0:T(8,128)S(1)}, f32[1,32]{1,0:T(1,128)S(1)}) custom-call(bf16[28,512]{1,0:T(8,128)(2,1)} %bitcast.3, s32[4,128]{1,0:T(4,128)} %bitcast.4, f32[28,32,50]{2,1,0:T(8,128)} %w_in.1, f32[32,50]{1,0:T(8,128)} %w_out.1, f32[28,32,50]{2,1,0:T(8,128)} %mom_in.1, ...), custom_call_target="tpu_custom_call" | custom-call | tf_op jit(solution)/shard_map/hmc/pallas_call | solution.py:337
  30.6 1.0 %store.1 = (f32[28,32,50]{2,1,0:T(8,128)}, f32[32,50]{1,0:T(8,128)}, f32[28,32,50]{2,1,0:T(8,128)}, f32[32,50]{1,0:T(8,128)}, f32[1,32]{1,0:T(1,128)}) custom-call(f32[28,32,50]{2,1,0:T(8,128)S(1)} %get-tuple-element.15.refs_0_, f32[32,50]{1,0:T(8,128)S(1)} %get-tuple-element.16.refs_1_, f32[28,32,50]{2,1,0:T(8,128)S(1)} %get-tuple-element.17.refs_2_, ...), custom_call_target="tpu_custom_call" | custom-call | tf_op jit(solution)/shard_map/store/pallas_call | solution.py:357

commit v6 on v5

--- a/solution.py
+++ b/solution.py
@@ -148,7 +148,7 @@
         p2[g, rows, :] = p
         w2[g, rows, :] = w + f * p
 
-    def slots(final, e_prev, f_prev, e_now, f_now, after1=None, after0=None):
+    def slots(final, e_prev, f_prev, e_now, f_now, hooks={}):
         ahead = {}
         grad = None
         for s in range(U):
@@ -165,13 +165,11 @@
             if s == LAG - 1:
                 update(1, grad, e_prev, f_prev)
                 grad = None
-                if after1 is not None:
-                    after1()
             elif s == NC + LAG - 1:
                 update(0, grad, e_now, f_now)
                 grad = None
-                if after0 is not None:
-                    after0()
+            for hook in hooks.get(s, ()):
+                hook()
         return ahead, grad
 
     for k in range(LEAD):
@@ -235,9 +233,9 @@
         quad = quad + pltpu.roll(quad, 4, 0)
         return jnp.sum(loss, axis=1, keepdims=True) + 0.5 * quad
 
-    def send_momenta(g, to):
+    def pack_momenta(g):
+        pack(g, p1, p2, packp)
         packp[g, pl.ds(56, 4), pl.ds(64, 64)] = energy(g)[0:4, 0:64]
-        return send(g, packp, recvp, sp, rp, to)
 
     sent = {}
 
@@ -245,22 +243,27 @@
         pack(0, w1, w2, packw)
         sent["w0"] = send(0, packw, recvw, sw, rw, (2, 1))
 
+    def pack_w1():
+        pack(1, w1, w2, packw)
+
     def send_w1():
-        pack(1, w1, w2, packw)
         sent["w1"] = send(1, packw, recvw, sw, rw, (2, 1))
 
+    def pack_p0():
+        pack_momenta(0)
+
     def send_p0():
-        pack(0, p1, p2, packp)
-        sent["p0"] = send_momenta(0, (2, 1))
+        sent["p0"] = send(0, packp, recvp, sp, rp, (2, 1))
 
     send_w0()
-    ahead, grad = slots(True, eps, eps, half, 0.0, send_w1, send_p0)
+    ahead, grad = slots(True, eps, eps, half, 0.0,
+                        {LAG - 1: (pack_w1,), LAG + 2: (send_w1,), NC + LAG - 1: (pack_p0,), U - 2: (send_p0,)})
     for u in range(U - LAG, U):
         backward(u, resid(u))
         grad = grad + mm_grad(u)
     update(1, grad, half, 0.0)
-    pack(1, p1, p2, packp)
-    sent["p1"] = send_momenta(1, (2, 3, 1))
+    pack_momenta(1)
+    sent["p1"] = send(1, packp, recvp, sp, rp, (2, 3, 1))
 
     lane1 = lax.broadcasted_iota(jnp.int32, (1, 128), 1)
 

time: 31.7 us -> 31.5 us (level)
  no operation moved by 1% of the time
where the time goes in v6:
time: 31.5 us; the launch traced here: 31.4 us
  Pallas kernels  30.8 us (98%)
  between operations  0.64 us (2%)
    pallas_call x1, Pallas kernels, device_body(): pl.pallas_call(functools.partial(kernel, dims), name='hmc', out_shape=[S(...  29.8 us
    pallas_call x1, Pallas kernels, device_body(): pl.pallas_call(store_kernel, name='store', out_shape=[S(o.shape, o.dtype)...  0.97 us

profile of v6, /device:TPU:0, one launch (start us, length us, event | category | flops | bytes accessed | tf_op | source)
XLA Modules:
  0.0 31.4 jit_solution(7880453974066817962)
XLA Ops:
  0.6 29.8 %hmc.1 = (f32[28,32,50]{2,1,0:T(8,128)S(1)}, f32[32,50]{1,0:T(8,128)S(1)}, f32[28,32,50]{2,1,0:T(8,128)S(1)}, f32[32,50]{1,0:T(8,128)S(1)}, f32[1,32]{1,0:T(1,128)S(1)}) custom-call(bf16[28,512]{1,0:T(8,128)(2,1)} %bitcast.3, s32[4,128]{1,0:T(4,128)} %bitcast.4, f32[28,32,50]{2,1,0:T(8,128)} %w_in.1, f32[32,50]{1,0:T(8,128)} %w_out.1, f32[28,32,50]{2,1,0:T(8,128)} %mom_in.1, ...), custom_call_target="tpu_custom_call" | custom-call | tf_op jit(solution)/shard_map/hmc/pallas_call | solution.py:340
  30.4 1.0 %store.1 = (f32[28,32,50]{2,1,0:T(8,128)}, f32[32,50]{1,0:T(8,128)}, f32[28,32,50]{2,1,0:T(8,128)}, f32[32,50]{1,0:T(8,128)}, f32[1,32]{1,0:T(1,128)}) custom-call(f32[28,32,50]{2,1,0:T(8,128)S(1)} %get-tuple-element.15.refs_0_, f32[32,50]{1,0:T(8,128)S(1)} %get-tuple-element.16.refs_1_, f32[28,32,50]{2,1,0:T(8,128)S(1)} %get-tuple-element.17.refs_2_, ...), custom_call_target="tpu_custom_call" | custom-call | tf_op jit(solution)/shard_map/store/pallas_call | solution.py:360
